TPU v7x, 32 devices: a whole 2x2x4 slice. The times are simulated.
32 devices in a mesh: row: 4 (over x, core), col: 8 (over z, y).
Axes of the slice: x: 2, y: 2, z: 4, core: 2. Of those that a mesh axis runs over, the one named last changes fastest.
Arguments:
- panel: bfloat16 [32768, 512], P('row', 'col'), may hold values from -0.03125 to 0.03125
- pheno: bfloat16 [32768, 2048], P('row', 'col'), may hold values from -48 to 48
- kin_values: float32 [512], replicated, may hold values from 0.1 to 10
- trait_values: float32 [128], replicated, may hold values from 0.1 to 10
- trait_basis: float32 [128, 128], replicated, may hold values from -0.5 to 0.5
Outputs:
- coeffs: float32 [512, 2048], P('row', 'col')
- genetic: bfloat16 [32768, 2048], P('row', 'col')
All inputs are finite; a program needn't handle non-finite values.
Results may differ from a plain program's by a relative error of at most 0.0049.
Values may be sent and summed in bfloat16 or wider, within the bound.
A program may use at most 64 MiB of HBM per device.

v0:
```python
import jax
import jax.numpy as jnp
from jax import lax
from jax.sharding import PartitionSpec as P

TRAITS = 128
SETS_DEV = 2


def local(panel, pheno, kin_values, trait_values, trait_basis):
    col_count = lax.axis_size("col")
    columns = pheno.shape[1]
    traits_here = TRAITS // col_count
    set_count = SETS_DEV * col_count
    whole_panel = lax.all_gather(panel, "col", axis=1, tiled=True)
    partial_value = lax.dot_general(
        whole_panel, pheno, (((0,), (0,)), ((), ())), preferred_element_type=jnp.float32
    )
    summed = lax.psum_scatter(partial_value, "row", scatter_dimension=0, tiled=True)
    first_row = lax.axis_index("row") * summed.shape[0]
    share_rows = summed.shape[0]
    by_trait = summed.reshape(share_rows, traits_here, set_count).transpose(0, 2, 1)
    by_trait = by_trait.reshape(share_rows, set_count * traits_here)
    grouped = lax.all_to_all(by_trait, "col", split_axis=1, concat_axis=1, tiled=True)
    grouped = grouped.reshape(share_rows, col_count, SETS_DEV, traits_here).transpose(0, 2, 1, 3)
    grouped = grouped.reshape(share_rows, SETS_DEV, TRAITS)
    rotated = jnp.einsum("rst,tj->rsj", grouped, trait_basis, precision=lax.Precision.HIGHEST)
    kin_rows = lax.dynamic_slice_in_dim(kin_values, first_row, share_rows, 0)
    product = kin_rows[:, None] * trait_values[None, :]
    scaled = rotated * (product / (product + 1.0))[:, None, :]
    unrotated = jnp.einsum("rsj,tj->rst", scaled, trait_basis, precision=lax.Precision.HIGHEST)
    outgoing = unrotated.reshape(share_rows, SETS_DEV, col_count, traits_here).transpose(0, 2, 1, 3)
    outgoing = outgoing.reshape(share_rows, col_count * SETS_DEV * traits_here)
    returned = lax.all_to_all(outgoing, "col", split_axis=1, concat_axis=1, tiled=True)
    coeffs = returned.reshape(share_rows, set_count, traits_here).transpose(0, 2, 1)
    coeffs = coeffs.reshape(share_rows, columns)
    coeffs_low = lax.all_gather(coeffs.astype(jnp.bfloat16), "row", axis=0, tiled=True)
    genetic = jnp.dot(whole_panel, coeffs_low, preferred_element_type=jnp.float32)
    return (coeffs, genetic.astype(jnp.bfloat16))


def solution(mesh):
    return jax.shard_map(
        local,
        mesh=mesh,
        in_specs=(P("row", "col"), P("row", "col"), P(), P(), P()),
        out_specs=(P("row", "col"), P("row", "col")),
        check_vma=False,
    )
```

profile of v0, /device:TPU:1, one launch (start us, length us, event | category | flops | bytes accessed | tf_op | source)
XLA Modules:
  0.0 217.4 jit_solution(12070985339430566774)
XLA Ops:
  7.2 0.0 copy-start
  7.2 0.0 all-gather.2.cloned.1.call-start
  7.2 0.7 all-gather.2.cloned.1.call-update
  7.9 0.0 copy-start.1
  7.9 0.0 reduce-scatter.2.cloned.1.call-start
  8.0 128.0 %all-gather.2.cloned.1.call-done = bf16[8192,512]{0,1:T(8,128)(2,1)} async-done(((bf16[8192,64]{0,1:T(8,128)(2,1)}), bf16[8192,512]{0,1:T(8,128)(2,1)}) %all-gather.2.cloned.1.call-update) | async-done | bytes 8388624 | tf_op jit(solution)/shard_map/all_gather | solution.py:15
  136.0 7.7 %fusion.4 = f32[512,256]{1,0:T(8,128)} fusion(bf16[8192,512]{0,1:T(8,128)(2,1)} %all-gather.2.cloned.1.call-done, bf16[8192,256]{1,0:T(8,128)(2,1)} %param.6), kind=kOutput, calls=%fused_computation.8 | convolution fusion | flops 2147483648 | bytes 13107200 | tf_op jit(solution)/shard_map/dot_general | solution.py:16
  143.7 0.0 reduce-scatter.2.cloned.1.call-update
  143.7 20.5 %reduce-scatter.2.cloned.1.call-done = f32[128,256]{1,0:T(8,128)} async-done(((f32[512,256]{1,0:T(8,128)}), f32[128,256]{1,0:T(8,128)}) %reduce-scatter.2.cloned.1.call-update) | async-done | bytes 131088 | tf_op jit(solution)/shard_map/reduce_scatter | solution.py:19
  164.2 1.0 copy.8
  165.2 0.7 copy.9
  165.9 5.2 %all-to-all-start = ((f32[128,8,32]{0,2,1:T(8,128)}), f32[128,8,32]{0,2,1:T(8,128)S(1)}, u32[]{:S(2)}, u32[]{:S(2)}) async-start(f32[128,8,32]{0,2,1:T(8,128)} %bitcast.2), calls=%async_computation.1 | async-start | bytes 262144 | tf_op jit(solution)/shard_map/all_to_all | solution.py:24
  171.2 0.8 dynamic_slice.3
  171.9 0.0 copy-done.1
  171.9 0.1 add_divide_fusion
  172.0 5.4 %all-to-all-done = f32[128,8,32]{0,2,1:T(8,128)S(1)} async-done(((f32[128,8,32]{0,2,1:T(8,128)}), f32[128,8,32]{0,2,1:T(8,128)S(1)}, u32[]{:S(2)}, u32[]{:S(2)}) %all-to-all-start) | async-done | bytes 131104 | tf_op jit(solution)/shard_map/all_to_all | solution.py:24
  177.5 0.0 copy-done
  177.5 0.4 convolution_multiply_fusion
  177.9 0.3 fusion.1
  178.2 8.6 %all_to_all.18 = f32[128,8,32]{0,2,1:T(8,128)S(1)} all-to-all(f32[128,8,32]{0,2,1:T(8,128)S(1)} %bitcast.35), channel_id=1, replica_groups=mesh['row'=4,'col'=8] {'col'}, dimensions={1} | all-to-all | bytes 262144 | tf_op jit(solution)/shard_map/all_to_all | solution.py:34
  186.8 0.8 copy.13
  187.6 8.9 %all_gather.7 = bf16[512,256]{0,1:T(8,128)(2,1)S(1)} all-gather(bf16[128,256]{0,1:T(8,128)(2,1)S(1)} %bitcast_convert_fusion), channel_id=1, replica_groups=mesh['row'=4,'col'=8] {'row'}, dimensions={0}, use_global_device_ids=true | all-gather | bytes 327680 | tf_op jit(solution)/shard_map/all_gather | solution.py:37
  196.5 7.7 %fusion = bf16[8192,256]{0,1:T(8,128)(2,1)} fusion(bf16[512,256]{0,1:T(8,128)(2,1)S(1)} %all_gather.7, bf16[8192,512]{0,1:T(8,128)(2,1)} %all-gather.2.cloned.1.call-done), kind=kOutput, calls=%fused_computation.1 | convolution fusion | flops 2149580800 | bytes 12845056 | tf_op jit(solution)/shard_map/dot_general | solution.py:38
  204.2 6.4 %copy.14 = bf16[8192,256]{1,0:T(8,128)(2,1)} copy(bf16[8192,256]{0,1:T(8,128)(2,1)} %fusion) | data formatting | bytes 8388608
  (4 shorter events, 0.1 us)
Async XLA Ops:
  7.2 170.3 %copy-start = (f32[128,128]{1,0:T(8,128)S(1)}, f32[128,128]{1,0:T(8,128)}, u32[]{:S(2)}) copy-start(f32[128,128]{1,0:T(8,128)} %param.9) | copy-start | bytes 196612
  7.2 128.8 %all-gather.2.cloned.1.call-start = ((), (), s32[]{:S(2)}) async-start(), calls=%async_computation.3 | async-start | bytes 9437184 | tf_op jit(solution)/shard_map/all_gather | solution.py:15
  7.9 164.0 %copy-start.1 = (f32[128]{0:T(128)S(1)}, f32[128]{0:T(128)}, u32[]{:S(2)}) copy-start(f32[128]{0:T(128)} %param.8) | copy-start | bytes 1540
  7.9 156.3 %reduce-scatter.2.cloned.1.call-start = ((), (), s32[]{:S(2)}) async-start(), calls=%async_computation.4 | async-start | bytes 655360 | tf_op jit(solution)/shard_map/reduce_scatter | solution.py:19
  165.9 11.5 %all-to-all-start = ((f32[128,8,32]{0,2,1:T(8,128)}), f32[128,8,32]{0,2,1:T(8,128)S(1)}, u32[]{:S(2)}, u32[]{:S(2)}) async-start(f32[128,8,32]{0,2,1:T(8,128)} %bitcast.2), calls=%async_computation.1 | async-start | bytes 262144 | tf_op jit(solution)/shard_map/all_to_all | solution.py:24
Sparse Core Ops, SparseCore 0:
  10.1 125.8 all-gather.1
  143.8 20.3 reduce-scatter.1
where the time goes:
time: 218 us; the launch traced here: 217 us
  waiting for transfers between devices  155 us (71%)
  blocking collectives  17.5 us (8%)
  matrix products  16.1 us (7%)
  between operations  14.1 us (6%)
  local copies, waits for them, and re-layouts  9.64 us (4%)
  starting transfers between devices  5.33 us (2%)
    all_gather x1, waiting for transfers between devices, local(): whole_panel = lax.all_gather(panel, 'col', axis=1, tiled=True)  128 us
    reduce_scatter x1, waiting for transfers between devices, local(): lax.psum_scatter(partial_value, 'row', scatter_dimension=0, tiled=True)  20.5 us
    all_gather x1, blocking collectives, local(): lax.all_gather(coeffs.astype(jnp.bfloat16), 'row', axis=0, tiled=True)  8.92 us
    all_to_all x1, blocking collectives, local(): lax.all_to_all(outgoing, 'col', split_axis=1, concat_axis=1, tiled=True)  8.59 us
    dot_general x1, matrix products, local(): lax.dot_general(whole_panel, pheno, (((0,), (0,)), ((), ())), preferred_e...  7.7 us
    dot_general x1, matrix products, local(): jnp.dot(whole_panel, coeffs_low, preferred_element_type=jnp.float32)  7.69 us
    unnamed x6, local copies, waits for them, and re-layouts  7.13 us
    all_to_all x1, waiting for transfers between devices, local(): lax.all_to_all(by_trait, 'col', split_axis=1, concat_axis=1, tiled=True)  5.44 us
  transfers between devices with their start and end apart: 3, of which 3 were waited for; matrix products, arithmetic and copies ran while one was open for 0% of the time, Pallas kernels for 0%

commit v1 on v0

v1 whole, which is shorter than its diff:
```python
import functools

import jax
import jax.numpy as jnp
from jax import lax
from jax.experimental import pallas as pl
from jax.experimental.pallas import tpu as pltpu
from jax.sharding import PartitionSpec as P

LANES = 128
PIECES = 4
MESH = pl.DeviceIdType.MESH
HIGH = lax.Precision.HIGHEST


def gather_rotate(
    rows, cols, q, pheno, basis, basis_t, kin, trait,
    g_out, c_out, coeffs_out,
    g, ph, pht, acc, part_f, part, rparts, sb, rb, ob, crow, ct,
    load_sem, send_sem, recv_sem, out_sem, rs_send, rs_recv, a1_send, a1_recv, a2_send, a2_recv, ag_send, ag_recv,
):
    me_r, me_c = lax.axis_index("row"), lax.axis_index("col")
    lines = cols // 2
    z, y = me_c // 2, lax.rem(me_c, 2)
    other = me_c + 1 - 2 * y
    half_ind = q.shape[0]
    piece = half_ind // PIECES
    columns = pheno.shape[1]
    traits = basis.shape[0]
    sets = columns * cols // traits
    t_here = traits // cols
    width = LANES // 2

    own_load = pltpu.make_async_copy(q, g.at[me_c], load_sem.at[0])
    own_load.start()
    ph_load = pltpu.make_async_copy(pheno, ph, load_sem.at[1])
    ph_load.start()

    barrier = pltpu.get_barrier_semaphore()
    for d in range(1, cols):
        pl.semaphore_signal(barrier, inc=1, device_id=(me_r, lax.rem(me_c + d, cols)), device_id_type=MESH)
    for d in range(1, rows):
        pl.semaphore_signal(barrier, inc=1, device_id=(lax.rem(me_r + d, rows), me_c), device_id_type=MESH)
    pl.semaphore_wait(barrier, cols + rows - 2)

    def hop(way, block, j):
        target = (jnp.minimum(me_c + 2, cols - 2 + y), jnp.maximum(me_c - 2, y), other)[way]
        here = g.at[block, pl.ds(j * piece, piece)]
        return pltpu.make_async_remote_copy(
            src_ref=here, dst_ref=here,
            send_sem=send_sem.at[way, block, j], recv_sem=recv_sem.at[block, j],
            device_id=(me_r, target), device_id_type=MESH,
        )

    def arrived(block, j):
        hop(2, block, j).wait_recv()

    up, down = z < lines - 1, z > 0
    late = PIECES // 2

    def line_sends(block, j, act):
        @pl.when(up)
        def _():
            act(hop(0, block, j))

        @pl.when(down)
        def _():
            act(hop(1, block, j))

    own_load.wait()
    for j in range(PIECES):
        line_sends(me_c, j, lambda h: h.start())
        hop(2, me_c, j).start()

    ph_load.wait()
    tile = 256

    def turn(i, _):
        for h in range(2):
            at = pl.multiple_of(h * half_ind + i * tile, tile)
            pht[h * columns:(h + 1) * columns, pl.ds(pl.multiple_of(i * tile, tile), tile)] = ph[pl.ds(at, tile), :].T
        return 0

    lax.fori_loop(0, half_ind // tile, turn, 0)

    def project(pair):
        mine, theirs = 2 * pair + y, 2 * pair + 1 - y
        for b in (2 * pair, 2 * pair + 1):
            pltpu.make_async_copy(g.at[b], g_out.at[b], out_sem.at[b]).start()
        acc[...] = jnp.zeros_like(acc)
        step = 1024

        def add(i, _):
            at = pl.ds(pl.multiple_of(i * step, step), step)
            rhs = jnp.concatenate([g[2 * pair, at, :], g[2 * pair + 1, at, :]], axis=1)
            acc[...] += jnp.dot(pht[:, at], rhs, preferred_element_type=jnp.float32)
            return 0

        lax.fori_loop(0, half_ind // step, add, 0)
        lane = lax.broadcasted_iota(jnp.int32, (columns, LANES), 1)
        low = lane < width
        top, bottom = acc[:columns, :], acc[columns:, :]
        first = top[:, :LANES] + pltpu.roll(bottom[:, :LANES], width, 1)
        second = pltpu.roll(top[:, LANES:], width, 1) + bottom[:, LANES:]
        part_f[...] = jnp.where(low, first, second)
        for s in range(sets):
            part[pair, s * t_here:(s + 1) * t_here, :] = part_f[pl.ds(s, t_here, stride=sets), :].astype(jnp.bfloat16)

        @pl.when(pair != me_r)
        def _():
            reduce_copy(pair).start()

    def reduce_copy(pair):
        return pltpu.make_async_remote_copy(
            src_ref=part.at[pair], dst_ref=rparts.at[me_r],
            send_sem=rs_send.at[pair], recv_sem=rs_recv.at[me_r],
            device_id=(pair, me_c), device_id_type=MESH,
        )

    def wait_theirs(pair):
        for j in range(PIECES):
            arrived(2 * pair + 1 - y, j)

    def around(s, fn):
        @pl.when(z - s >= 0)
        def _():
            fn(z - s)

        @pl.when(z + s < lines)
        def _():
            fn(z + s)

    def late_round(pair):
        wait_theirs(pair)
        project(pair)

    for s in range(1, lines):
        for j in range(PIECES):
            skip = s == 1 and j >= late

            @pl.when(z - s >= 0)
            def _():
                b = me_c - 2 * s
                arrived(b, j)

                @pl.when(up)
                def _():
                    hop(0, b, j).start()

                if not skip:
                    hop(2, b, j).start()

            @pl.when(z + s < lines)
            def _():
                b = me_c + 2 * s
                arrived(b, j)

                @pl.when(down)
                def _():
                    hop(1, b, j).start()

                if not skip:
                    hop(2, b, j).start()

        if s == 1:
            wait_theirs(z)
            project(z)
    for j in range(late, PIECES):
        line_sends(other, j, lambda h: h.start())
    for s in list(range(2, lines)) + [1]:
        around(s, late_round)

    total = part[me_r].astype(jnp.float32)
    for d in range(1, rows):
        src = lax.rem(me_r + d, rows)
        pltpu.make_async_remote_copy(
            src_ref=part.at[src], dst_ref=rparts.at[src], send_sem=rs_send.at[src], recv_sem=rs_recv.at[src],
            device_id=(src, me_c), device_id_type=MESH,
        ).wait_recv()
        total = total + rparts[src].astype(jnp.float32)
    sb[...] = total.astype(jnp.bfloat16).reshape(sb.shape)

    def trade1(peer, slot):
        return pltpu.make_async_remote_copy(
            src_ref=sb.at[peer], dst_ref=rb.at[slot], send_sem=a1_send.at[peer], recv_sem=a1_recv.at[slot],
            device_id=(me_r, peer), device_id_type=MESH,
        )

    def trade2(peer, slot):
        return pltpu.make_async_remote_copy(
            src_ref=ob.at[peer], dst_ref=crow.at[me_r, slot], send_sem=a2_send.at[peer], recv_sem=a2_recv.at[slot],
            device_id=(me_r, peer), device_id_type=MESH,
        )

    def share(peer, slot):
        return pltpu.make_async_remote_copy(
            src_ref=crow.at[me_r], dst_ref=crow.at[slot], send_sem=ag_send.at[peer], recv_sem=ag_recv.at[slot],
            device_id=(peer, me_c), device_id_type=MESH,
        )

    col_peers = [lax.rem(me_c + d, cols) for d in range(1, cols)]
    row_peers = [lax.rem(me_r + d, rows) for d in range(1, rows)]
    for p in col_peers:
        trade1(p, me_c).start()
    rb[me_c] = sb[me_c]
    product = kin[pl.ds(me_r, 1), :] * trait[...]
    weight = product / (product + 1.0)
    for p in col_peers:
        trade1(p, p).wait_recv()
    s_here = sets // cols
    got = jnp.concatenate(
        [rb[:, s * t_here:(s + 1) * t_here, :].astype(jnp.float32).reshape(traits, LANES) for s in range(s_here)], axis=1
    )
    rotated = jnp.dot(basis_t[...], got, precision=HIGH, preferred_element_type=jnp.float32)
    scaled = rotated * jnp.concatenate([weight] * s_here, axis=1)
    back = jnp.dot(basis[...], scaled, precision=HIGH, preferred_element_type=jnp.float32)
    for s in range(s_here):
        ob[:, s * t_here:(s + 1) * t_here, :] = (
            back[:, s * LANES:(s + 1) * LANES].reshape(cols, t_here, LANES).astype(jnp.bfloat16)
        )
    for p in col_peers:
        trade2(p, me_c).start()
    crow[me_r, me_c] = ob[me_c]
    for p in col_peers:
        trade2(p, p).wait_recv()
    for p in row_peers:
        share(p, me_r).start()

    def place(r):
        for s in range(sets):
            part_s = crow[r, s // s_here, (s % s_here) * t_here:(s % s_here + 1) * t_here, :]
            ct[pl.ds(s, t_here, stride=sets), :] = part_s.astype(jnp.float32)
        turned = ct[...].T
        c_out[pl.ds(pl.multiple_of(r * LANES, LANES), LANES), :] = turned.astype(jnp.bfloat16)
        return turned

    coeffs_out[...] = place(me_r)
    for p in row_peers:
        share(p, p).wait_recv()
        place(p)

    for j in range(PIECES):
        line_sends(me_c, j, lambda h: h.wait_send())
        hop(2, me_c, j).wait_send()
        if j >= late:
            line_sends(other, j, lambda h: h.wait_send())
        for s in range(1, lines):
            skip = s == 1 and j >= late

            @pl.when(z - s >= 0)
            def _():
                @pl.when(up)
                def _():
                    hop(0, me_c - 2 * s, j).wait_send()

                if not skip:
                    hop(2, me_c - 2 * s, j).wait_send()

            @pl.when(z + s < lines)
            def _():
                @pl.when(down)
                def _():
                    hop(1, me_c + 2 * s, j).wait_send()

                if not skip:
                    hop(2, me_c + 2 * s, j).wait_send()

    for p in row_peers:
        reduce_copy(p).wait_send()
        share(p, me_r).wait_send()
    for p in col_peers:
        trade1(p, me_c).wait_send()
        trade2(p, me_c).wait_send()
    for b in range(cols):
        pltpu.make_async_copy(g.at[b], g_out.at[b], out_sem.at[b]).wait()


def predict(g, c, out, wide):
    blocks = g.shape[0]
    width = LANES // 2
    columns = c.shape[1]

    @pl.when(pl.program_id(0) == 0)
    def _():
        wide[...] = jnp.zeros_like(wide)
        for k in range(blocks):
            rows = c[k * width:(k + 1) * width, :]
            wide[k * LANES:k * LANES + width, :columns] = rows
            wide[k * LANES + width:(k + 1) * LANES, columns:] = rows

    lhs = jnp.concatenate([g[k] for k in range(blocks)], axis=1)
    res = jnp.dot(lhs, wide[...], preferred_element_type=jnp.float32).astype(jnp.bfloat16)
    out[0] = res[:, :columns]
    out[1] = res[:, columns:]


def fused(panel, pheno, kin_values, trait_values, trait_basis):
    rows, cols = lax.axis_size("row"), lax.axis_size("col")
    ind, columns = pheno.shape
    half = ind // 2
    traits = trait_basis.shape[0]
    sets = columns * cols // traits
    share = kin_values.shape[0] // rows
    q = jnp.concatenate([panel[:half], panel[half:]], axis=1)
    bf, f32 = jnp.bfloat16, jnp.float32
    hbm = pl.BlockSpec(memory_space=pltpu.HBM)
    vmem = pl.BlockSpec(memory_space=pltpu.VMEM)
    lot = columns // cols
    dma = pltpu.SemaphoreType.DMA
    g, c, coeffs = pl.pallas_call(
        functools.partial(gather_rotate, rows, cols),
        out_shape=(
            jax.ShapeDtypeStruct((cols, half, LANES), bf),
            jax.ShapeDtypeStruct((rows * share, columns), bf),
            jax.ShapeDtypeStruct((share, columns), f32),
        ),
        in_specs=[hbm, hbm, vmem, vmem, vmem, vmem],
        out_specs=(hbm, vmem, vmem),
        scratch_shapes=[
            pltpu.VMEM((cols, half, LANES), bf),
            pltpu.VMEM((ind, columns), bf),
            pltpu.VMEM((2 * columns, half), bf),
            pltpu.VMEM((2 * columns, 2 * LANES), f32),
            pltpu.VMEM((columns, LANES), f32),
            pltpu.VMEM((rows, columns, LANES), bf),
            pltpu.VMEM((rows, columns, LANES), bf),
            pltpu.VMEM((cols, lot, LANES), bf),
            pltpu.VMEM((cols, lot, LANES), bf),
            pltpu.VMEM((cols, lot, LANES), bf),
            pltpu.VMEM((rows, cols, lot, LANES), bf),
            pltpu.VMEM((columns, LANES), f32),
            dma((2,)), dma((3, cols, PIECES)), dma((cols, PIECES)), dma((cols,)),
            dma((rows,)), dma((rows,)), dma((cols,)), dma((cols,)), dma((cols,)), dma((cols,)),
            dma((rows,)), dma((rows,)),
        ],
        compiler_params=pltpu.CompilerParams(
            collective_id=0, has_side_effects=True, vmem_limit_bytes=40 * 1024 * 1024
        ),
    )(q, pheno, trait_basis, trait_basis.T, kin_values.reshape(rows, share), trait_values[:, None])
    tile = 512
    genetic = pl.pallas_call(
        predict,
        out_shape=jax.ShapeDtypeStruct((2, half, columns), bf),
        grid=(half // tile,),
        in_specs=[
            pl.BlockSpec((cols, tile, LANES), lambda i: (0, i, 0)),
            pl.BlockSpec((rows * share, columns), lambda i: (0, 0)),
        ],
        out_specs=pl.BlockSpec((2, tile, columns), lambda i: (0, i, 0)),
        scratch_shapes=[pltpu.VMEM((cols * LANES, 2 * columns), bf)],
    )(g, c)
    return coeffs, genetic.reshape(ind, columns)


def local(panel, pheno, kin_values, trait_values, trait_basis):
    rows, cols = lax.axis_size("row"), lax.axis_size("col")
    eigen = kin_values.shape[0]
    if 2 * panel.shape[1] == LANES and eigen // rows == LANES and trait_basis.shape[0] // cols == 16:
        return fused(panel, pheno, kin_values, trait_values, trait_basis)
    return plain(panel, pheno, kin_values, trait_values, trait_basis)


def plain(panel, pheno, kin_values, trait_values, trait_basis):
    col_count = lax.axis_size("col")
    columns = pheno.shape[1]
    traits = trait_basis.shape[0]
    traits_here = traits // col_count
    set_count = columns // traits_here
    sets_dev = set_count // col_count
    whole_panel = lax.all_gather(panel, "col", axis=1, tiled=True)
    partial_value = lax.dot_general(
        whole_panel, pheno, (((0,), (0,)), ((), ())), preferred_element_type=jnp.float32
    )
    summed = lax.psum_scatter(partial_value, "row", scatter_dimension=0, tiled=True)
    first_row = lax.axis_index("row") * summed.shape[0]
    share_rows = summed.shape[0]
    by_trait = summed.reshape(share_rows, traits_here, set_count).transpose(0, 2, 1)
    by_trait = by_trait.reshape(share_rows, set_count * traits_here)
    grouped = lax.all_to_all(by_trait, "col", split_axis=1, concat_axis=1, tiled=True)
    grouped = grouped.reshape(share_rows, col_count, sets_dev, traits_here).transpose(0, 2, 1, 3)
    grouped = grouped.reshape(share_rows, sets_dev, traits)
    rotated = jnp.einsum("rst,tj->rsj", grouped, trait_basis, precision=HIGH)
    kin_rows = lax.dynamic_slice_in_dim(kin_values, first_row, share_rows, 0)
    product = kin_rows[:, None] * trait_values[None, :]
    scaled = rotated * (product / (product + 1.0))[:, None, :]
    unrotated = jnp.einsum("rsj,tj->rst", scaled, trait_basis, precision=HIGH)
    outgoing = unrotated.reshape(share_rows, sets_dev, col_count, traits_here).transpose(0, 2, 1, 3)
    outgoing = outgoing.reshape(share_rows, col_count * sets_dev * traits_here)
    returned = lax.all_to_all(outgoing, "col", split_axis=1, concat_axis=1, tiled=True)
    coeffs = returned.reshape(share_rows, set_count, traits_here).transpose(0, 2, 1)
    coeffs = coeffs.reshape(share_rows, columns)
    coeffs_low = lax.all_gather(coeffs.astype(jnp.bfloat16), "row", axis=0, tiled=True)
    genetic = jnp.dot(whole_panel, coeffs_low, preferred_element_type=jnp.float32)
    return (coeffs, genetic.astype(jnp.bfloat16))


def solution(mesh):
    return jax.shard_map(
        local,
        mesh=mesh,
        in_specs=(P("row", "col"), P("row", "col"), P(), P(), P()),
        out_specs=(P("row", "col"), P("row", "col")),
        check_vma=False,
    )
```

time: 218 us -> 131 us (0.60)
  waiting for transfers between devices: 155 us -> 0 us
  Pallas kernels: 0 us -> 119 us
  blocking collectives: 17.5 us -> 0 us
  matrix products: 16.1 us -> 0 us
  between operations: 14.1 us -> 0.72 us
  starting transfers between devices: 5.33 us -> 0 us
    all_gather x1 -> x0, waiting for transfers between devices: 128 us -> none  [local(): whole_panel = lax.all_gather(panel, 'col', axis=1, tiled=True)]
    pallas_call x0 -> x2, Pallas kernels: none -> 119 us  [the longest x1 108 us: fused(): pl.pallas_call(functools.partial(gather_rotate, rows, cols), out_shape=(j...]
    reduce_scatter x1 -> x0, waiting for transfers between devices: 20.5 us -> none  [local(): lax.psum_scatter(partial_value, 'row', scatter_dimension=0, tiled=True)]
    dot_general x4 -> x0, matrix products: 16.1 us -> none  [the longest x1 7.7 us: local(): lax.dot_general(whole_panel, pheno, (((0,), (0,)), ((), ())), preferred_e...]
    all_gather x1 -> x0, blocking collectives: 8.92 us -> none  [local(): lax.all_gather(coeffs.astype(jnp.bfloat16), 'row', axis=0, tiled=True)]
    all_to_all x1 -> x0, blocking collectives: 8.59 us -> none  [local(): lax.all_to_all(outgoing, 'col', split_axis=1, concat_axis=1, tiled=True)]
    all_to_all x1 -> x0, waiting for transfers between devices: 5.44 us -> none  [local(): lax.all_to_all(by_trait, 'col', split_axis=1, concat_axis=1, tiled=True)]
    all_to_all x1 -> x0, starting transfers between devices: 5.25 us -> none  [local(): lax.all_to_all(by_trait, 'col', split_axis=1, concat_axis=1, tiled=True)]
  transfers between devices with their start and end apart: 3 -> 0, of which waited for: 3 -> 0; matrix products, arithmetic and copies ran while one was open for 0% -> 0% of each run, Pallas kernels for 0% -> 0%
where the time goes in v1:
time: 131 us
  Pallas kernels  119 us (91%)
  local copies, waits for them, and re-layouts  10.8 us (8%)
    pallas_call x1, Pallas kernels, fused(): pl.pallas_call(functools.partial(gather_rotate, rows, cols), out_shape=(j...  108 us
    pallas_call x1, Pallas kernels, fused(): pl.pallas_call(predict, out_shape=jax.ShapeDtypeStruct((2, half, columns)...  10.3 us
    unnamed x14, local copies, waits for them, and re-layouts  8.74 us

profile of v1, /device:TPU:1, one launch (start us, length us, event | category | flops | bytes accessed | tf_op | source)
XLA Modules:
  0.0 130.8 jit_solution(14571829943576486664)
XLA Ops:
  0.6 0.8 copy.10.trait
  1.4 0.9 copy.9
  2.3 0.0 copy-start.2
  2.3 0.0 copy-start.4
  2.3 1.3 fusion
  3.7 0.5 copy.11
  4.2 0.5 copy.12
  4.7 0.6 pad_maximum_fusion.q
  5.3 0.0 copy-done.2
  5.3 0.0 copy-done.4
  5.3 0.0 copy-start.1
  5.3 2.2 %copy-done.1 = bf16[8192,256]{1,0:T(8,128)(2,1)S(1)} copy-done((bf16[8192,256]{1,0:T(8,128)(2,1)S(1)}, bf16[8192,256]{1,0:T(8,128)(2,1)}, u32[]{:S(2)}) %copy-start.1) | copy-done | bytes 4194328
  7.5 108.4 %shard_map.68 = (bf16[8,4096,128]{2,1,0:T(8,128)(2,1)S(1)}, bf16[512,256]{1,0:T(8,128)(2,1)S(1)}, f32[128,256]{1,0:T(8,128)S(1)}) custom-call(bf16[4096,128]{1,0:T(8,128)(2,1)S(1)} %pad_maximum_fusion.q, bf16[8192,256]{1,0:T(8,128)(2,1)S(1)} %copy-done.1, f32[128,128]{1,0:T(8,128)S(1)} %copy-done.2, f32[128,128]{1,0:T(8,128)S(1)} %bitcast.4, ...), custom_call_target="tpu_custom_call" | custom-call | tf_op jit(solution)/shard_map/pallas_call | solution.py:310
  115.9 0.0 copy-start
  115.9 3.2 %copy-done = bf16[8,4096,128]{2,1,0:T(8,128)(2,1)} copy-done((bf16[8,4096,128]{2,1,0:T(8,128)(2,1)}, bf16[8,4096,128]{2,1,0:T(8,128)(2,1)S(1)}, u32[]{:S(2)}) %copy-start) | copy-done | bytes 8388632
  119.2 0.0 copy-start.3
  119.2 0.7 copy-done.3
  119.9 10.3 %shard_map.69 = bf16[2,4096,256]{2,1,0:T(8,128)(2,1)} custom-call(bf16[8,4096,128]{2,1,0:T(8,128)(2,1)} %copy-done, bf16[512,256]{1,0:T(8,128)(2,1)} %copy-done.3), custom_call_target="tpu_custom_call" | custom-call | tf_op jit(solution)/shard_map/pallas_call | solution.py:341
  130.1 0.7 copy.14
Async XLA Ops:
  2.3 3.0 %copy-start.2 = (f32[128,128]{1,0:T(8,128)S(1)}, f32[128,128]{1,0:T(8,128)}, u32[]{:S(2)}) copy-start(f32[128,128]{1,0:T(8,128)} %basis.1) | copy-start | bytes 196612
  2.3 3.0 %copy-start.4 = (f32[512]{0:T(512)S(1)}, f32[512]{0:T(512)}, u32[]{:S(2)}) copy-start(f32[512]{0:T(512)} %param.7) | copy-start | bytes 6148
  5.3 2.2 %copy-start.1 = (bf16[8192,256]{1,0:T(8,128)(2,1)S(1)}, bf16[8192,256]{1,0:T(8,128)(2,1)}, u32[]{:S(2)}) copy-start(bf16[8192,256]{1,0:T(8,128)(2,1)} %pheno.1) | copy-start | bytes 12582916
  115.9 3.2 %copy-start = (bf16[8,4096,128]{2,1,0:T(8,128)(2,1)}, bf16[8,4096,128]{2,1,0:T(8,128)(2,1)S(1)}, u32[]{:S(2)}) copy-start(bf16[8,4096,128]{2,1,0:T(8,128)(2,1)S(1)} %get-tuple-element.6.g) | copy-start | bytes 25165828
  119.2 0.7 copy-start.3

commit v2 on v1

--- a/solution.py
+++ b/solution.py
@@ -14,22 +14,21 @@
 
 
 def gather_rotate(
-    rows, cols, q, pheno, basis, basis_t, kin, trait,
-    g_out, c_out, coeffs_out,
-    g, ph, pht, acc, part_f, part, rparts, sb, rb, ob, crow, ct,
-    load_sem, send_sem, recv_sem, out_sem, rs_send, rs_recv, a1_send, a1_recv, a2_send, a2_recv, ag_send, ag_recv,
+    rows, cols, q, pheno, basis, kin, trait,
+    gen_out, coeffs_out,
+    w_out, c_out, held, gen_sem, g, ph, acc, part_f, part, rparts, sb, rb, ob, crow, ct,
+    load_sem, send_sem, recv_sem, rs_send, rs_recv, a1_send, a1_recv, a2_send, a2_recv, ag_send, ag_recv,
 ):
     me_r, me_c = lax.axis_index("row"), lax.axis_index("col")
     lines = cols // 2
     z, y = me_c // 2, lax.rem(me_c, 2)
     other = me_c + 1 - 2 * y
-    half_ind = q.shape[0]
-    piece = half_ind // PIECES
+    width, people = q.shape
+    piece = width // PIECES
     columns = pheno.shape[1]
     traits = basis.shape[0]
     sets = columns * cols // traits
     t_here = traits // cols
-    width = LANES // 2
 
     own_load = pltpu.make_async_copy(q, g.at[me_c], load_sem.at[0])
     own_load.start()
@@ -73,42 +72,36 @@
         hop(2, me_c, j).start()
 
     ph_load.wait()
-    tile = 256
-
-    def turn(i, _):
-        for h in range(2):
-            at = pl.multiple_of(h * half_ind + i * tile, tile)
-            pht[h * columns:(h + 1) * columns, pl.ds(pl.multiple_of(i * tile, tile), tile)] = ph[pl.ds(at, tile), :].T
-        return 0
-
-    lax.fori_loop(0, half_ind // tile, turn, 0)
 
     def project(pair):
-        mine, theirs = 2 * pair + y, 2 * pair + 1 - y
-        for b in (2 * pair, 2 * pair + 1):
-            pltpu.make_async_copy(g.at[b], g_out.at[b], out_sem.at[b]).start()
         acc[...] = jnp.zeros_like(acc)
-        step = 1024
+        step = 2048
 
         def add(i, _):
             at = pl.ds(pl.multiple_of(i * step, step), step)
-            rhs = jnp.concatenate([g[2 * pair, at, :], g[2 * pair + 1, at, :]], axis=1)
-            acc[...] += jnp.dot(pht[:, at], rhs, preferred_element_type=jnp.float32)
+            lhs = jnp.concatenate([g[2 * pair, :, at], g[2 * pair + 1, :, at]], axis=0)
+            acc[...] += jnp.dot(lhs, ph[at, :], preferred_element_type=jnp.float32)
             return 0
 
-        lax.fori_loop(0, half_ind // step, add, 0)
-        lane = lax.broadcasted_iota(jnp.int32, (columns, LANES), 1)
-        low = lane < width
-        top, bottom = acc[:columns, :], acc[columns:, :]
-        first = top[:, :LANES] + pltpu.roll(bottom[:, :LANES], width, 1)
-        second = pltpu.roll(top[:, LANES:], width, 1) + bottom[:, LANES:]
-        part_f[...] = jnp.where(low, first, second)
+        lax.fori_loop(0, people // step, add, 0)
+        part_f[...] = acc[...].T
         for s in range(sets):
             part[pair, s * t_here:(s + 1) * t_here, :] = part_f[pl.ds(s, t_here, stride=sets), :].astype(jnp.bfloat16)
 
         @pl.when(pair != me_r)
         def _():
             reduce_copy(pair).start()
+
+    def lay(pair):
+        step = 512
+        lanes = pl.ds(pl.multiple_of(pair * LANES, LANES), LANES)
+
+        def turn(i, _):
+            at = pl.ds(pl.multiple_of(i * step, step), step)
+            w_out[at, lanes] = jnp.concatenate([g[2 * pair, :, at], g[2 * pair + 1, :, at]], axis=0).T
+            return 0
+
+        lax.fori_loop(0, people // step, turn, 0)
 
     def reduce_copy(pair):
         return pltpu.make_async_remote_copy(
@@ -165,10 +158,15 @@
         if s == 1:
             wait_theirs(z)
             project(z)
+            lay(z)
     for j in range(late, PIECES):
         line_sends(other, j, lambda h: h.start())
-    for s in list(range(2, lines)) + [1]:
+    for s in range(2, lines - 1):
         around(s, late_round)
+        around(s, lay)
+    for s in (lines - 1, 1):
+        around(s, late_round)
+    around(lines - 1, lay)
 
     total = part[me_r].astype(jnp.float32)
     for d in range(1, rows):
@@ -203,7 +201,8 @@
     for p in col_peers:
         trade1(p, me_c).start()
     rb[me_c] = sb[me_c]
-    product = kin[pl.ds(me_r, 1), :] * trait[...]
+    around(1, lay)
+    product = kin[pl.ds(me_r, 1), :] * jnp.broadcast_to(trait[...], (LANES, traits)).T
     weight = product / (product + 1.0)
     for p in col_peers:
         trade1(p, p).wait_recv()
@@ -211,7 +210,7 @@
     got = jnp.concatenate(
         [rb[:, s * t_here:(s + 1) * t_here, :].astype(jnp.float32).reshape(traits, LANES) for s in range(s_here)], axis=1
     )
-    rotated = jnp.dot(basis_t[...], got, precision=HIGH, preferred_element_type=jnp.float32)
+    rotated = jnp.dot(basis[...].T, got, precision=HIGH, preferred_element_type=jnp.float32)
     scaled = rotated * jnp.concatenate([weight] * s_here, axis=1)
     back = jnp.dot(basis[...], scaled, precision=HIGH, preferred_element_type=jnp.float32)
     for s in range(s_here):
@@ -239,6 +238,21 @@
         share(p, p).wait_recv()
         place(p)
 
+    tiles = gen_sem.shape[0]
+    size = people // tiles
+
+    def emit(i):
+        at = pl.ds(pl.multiple_of(i * size, size), size)
+        return pltpu.make_async_copy(held.at[at], gen_out.at[at], gen_sem.at[i])
+
+    def predict(i, _):
+        at = pl.ds(pl.multiple_of(i * size, size), size)
+        held[at, :] = jnp.dot(w_out[at, :], c_out[...], preferred_element_type=jnp.float32).astype(jnp.bfloat16)
+        emit(i).start()
+        return 0
+
+    lax.fori_loop(0, tiles, predict, 0)
+
     for j in range(PIECES):
         line_sends(me_c, j, lambda h: h.wait_send())
         hop(2, me_c, j).wait_send()
@@ -271,56 +285,41 @@
     for p in col_peers:
         trade1(p, me_c).wait_send()
         trade2(p, me_c).wait_send()
-    for b in range(cols):
-        pltpu.make_async_copy(g.at[b], g_out.at[b], out_sem.at[b]).wait()
-
-
-def predict(g, c, out, wide):
-    blocks = g.shape[0]
-    width = LANES // 2
-    columns = c.shape[1]
-
-    @pl.when(pl.program_id(0) == 0)
-    def _():
-        wide[...] = jnp.zeros_like(wide)
-        for k in range(blocks):
-            rows = c[k * width:(k + 1) * width, :]
-            wide[k * LANES:k * LANES + width, :columns] = rows
-            wide[k * LANES + width:(k + 1) * LANES, columns:] = rows
-
-    lhs = jnp.concatenate([g[k] for k in range(blocks)], axis=1)
-    res = jnp.dot(lhs, wide[...], preferred_element_type=jnp.float32).astype(jnp.bfloat16)
-    out[0] = res[:, :columns]
-    out[1] = res[:, columns:]
+
+    def finish(i, _):
+        emit(i).wait()
+        return 0
+
+    lax.fori_loop(0, tiles, finish, 0)
 
 
 def fused(panel, pheno, kin_values, trait_values, trait_basis):
     rows, cols = lax.axis_size("row"), lax.axis_size("col")
     ind, columns = pheno.shape
-    half = ind // 2
     traits = trait_basis.shape[0]
     sets = columns * cols // traits
     share = kin_values.shape[0] // rows
-    q = jnp.concatenate([panel[:half], panel[half:]], axis=1)
     bf, f32 = jnp.bfloat16, jnp.float32
     hbm = pl.BlockSpec(memory_space=pltpu.HBM)
     vmem = pl.BlockSpec(memory_space=pltpu.VMEM)
     lot = columns // cols
     dma = pltpu.SemaphoreType.DMA
-    g, c, coeffs = pl.pallas_call(
+    genetic, coeffs = pl.pallas_call(
         functools.partial(gather_rotate, rows, cols),
         out_shape=(
-            jax.ShapeDtypeStruct((cols, half, LANES), bf),
-            jax.ShapeDtypeStruct((rows * share, columns), bf),
+            jax.ShapeDtypeStruct((ind, columns), bf),
             jax.ShapeDtypeStruct((share, columns), f32),
         ),
-        in_specs=[hbm, hbm, vmem, vmem, vmem, vmem],
-        out_specs=(hbm, vmem, vmem),
+        in_specs=[hbm, hbm, vmem, vmem, vmem],
+        out_specs=(hbm, vmem),
         scratch_shapes=[
-            pltpu.VMEM((cols, half, LANES), bf),
+            pltpu.VMEM((ind, rows * share), bf),
+            pltpu.VMEM((rows * share, columns), bf),
             pltpu.VMEM((ind, columns), bf),
-            pltpu.VMEM((2 * columns, half), bf),
-            pltpu.VMEM((2 * columns, 2 * LANES), f32),
+            dma((16,)),
+            pltpu.VMEM((cols, panel.shape[1], ind), bf),
+            pltpu.VMEM((ind, columns), bf),
+            pltpu.VMEM((share, columns), f32),
             pltpu.VMEM((columns, LANES), f32),
             pltpu.VMEM((rows, columns, LANES), bf),
             pltpu.VMEM((rows, columns, LANES), bf),
@@ -329,27 +328,15 @@
             pltpu.VMEM((cols, lot, LANES), bf),
             pltpu.VMEM((rows, cols, lot, LANES), bf),
             pltpu.VMEM((columns, LANES), f32),
-            dma((2,)), dma((3, cols, PIECES)), dma((cols, PIECES)), dma((cols,)),
+            dma((2,)), dma((3, cols, PIECES)), dma((cols, PIECES)),
             dma((rows,)), dma((rows,)), dma((cols,)), dma((cols,)), dma((cols,)), dma((cols,)),
             dma((rows,)), dma((rows,)),
         ],
         compiler_params=pltpu.CompilerParams(
-            collective_id=0, has_side_effects=True, vmem_limit_bytes=40 * 1024 * 1024
+            collective_id=0, has_side_effects=True, vmem_limit_bytes=48 * 1024 * 1024
         ),
-    )(q, pheno, trait_basis, trait_basis.T, kin_values.reshape(rows, share), trait_values[:, None])
-    tile = 512
-    genetic = pl.pallas_call(
-        predict,
-        out_shape=jax.ShapeDtypeStruct((2, half, columns), bf),
-        grid=(half // tile,),
-        in_specs=[
-            pl.BlockSpec((cols, tile, LANES), lambda i: (0, i, 0)),
-            pl.BlockSpec((rows * share, columns), lambda i: (0, 0)),
-        ],
-        out_specs=pl.BlockSpec((2, tile, columns), lambda i: (0, i, 0)),
-        scratch_shapes=[pltpu.VMEM((cols * LANES, 2 * columns), bf)],
-    )(g, c)
-    return coeffs, genetic.reshape(ind, columns)
+    )(panel.T, pheno, trait_basis, kin_values.reshape(rows, share), trait_values[None, :])
+    return coeffs, genetic
 
 
 def local(panel, pheno, kin_values, trait_values, trait_basis):

time: 131 us -> 119 us (0.908)
  Pallas kernels: 119 us -> 112 us
  local copies, waits for them, and re-layouts: 10.8 us -> 6.06 us
    pallas_call x1 -> x0, Pallas kernels: 10.3 us -> none  [fused(): pl.pallas_call(predict, out_shape=jax.ShapeDtypeStruct((2, half, columns)...]
    pallas_call x1, Pallas kernels: 108 us -> 112 us  [fused(): pl.pallas_call(functools.partial(gather_rotate, rows, cols), out_shape=(j...]
    unnamed x14 -> x10, local copies, waits for them, and re-layouts: 8.74 us -> 6.06 us
where the time goes in v2:
time: 119 us
  Pallas kernels  112 us (94%)
  local copies, waits for them, and re-layouts  6.06 us (5%)
    pallas_call x1, Pallas kernels, fused(): pl.pallas_call(functools.partial(gather_rotate, rows, cols), out_shape=(j...  112 us
    unnamed x10, local copies, waits for them, and re-layouts  6.06 us

profile of v2, /device:TPU:1, one launch (start us, length us, event | category | flops | bytes accessed | tf_op | source)
XLA Modules:
  0.0 118.6 jit_solution(2561973581524475845)
XLA Ops:
  0.6 0.0 copy-start
  0.6 1.2 %copy-done = bf16[8192,64]{0,1:T(8,128)(2,1)S(1)} copy-done((bf16[8192,64]{0,1:T(8,128)(2,1)S(1)}, bf16[8192,64]{0,1:T(8,128)(2,1)}, u32[]{:S(2)}) %copy-start) | copy-done | bytes 1048600
  1.9 0.0 copy-start.1
  1.9 0.8 copy-done.1
  2.7 0.0 copy-start.2
  2.7 0.7 copy-done.2
  3.4 0.0 copy-start.3
  3.4 0.7 copy-done.3
  4.0 111.9 %shard_map.68 = (bf16[8192,256]{1,0:T(8,128)(2,1)S(1)}, f32[128,256]{1,0:T(8,128)S(1)}) custom-call(bf16[64,8192]{1,0:T(8,128)(2,1)S(1)} %bitcast.3, bf16[8192,256]{1,0:T(8,128)(2,1)} %pheno.1, f32[128,128]{1,0:T(8,128)S(1)} %copy-done.1, f32[4,128]{1,0:T(4,128)S(1)} %bitcast.4, f32[1,128]{1,0:T(1,128)S(1)} %bitcast.5), custom_call_target="tpu_custom_call" | custom-call | tf_op jit(solution)/shard_map/pallas_call | solution.py:307
  116.0 0.7 copy.9
  116.6 2.0 %copy.10 = bf16[8192,256]{1,0:T(8,128)(2,1)} copy(bf16[8192,256]{1,0:T(8,128)(2,1)S(1)} %get-tuple-element.9) | data formatting | bytes 8388608
Async XLA Ops:
  0.6 1.2 %copy-start = (bf16[8192,64]{0,1:T(8,128)(2,1)S(1)}, bf16[8192,64]{0,1:T(8,128)(2,1)}, u32[]{:S(2)}) copy-start(bf16[8192,64]{0,1:T(8,128)(2,1)} %param.5) | copy-start | bytes 3145732
  1.9 0.8 copy-start.1
  2.7 0.7 copy-start.2
  3.4 0.7 copy-start.3

commit v3 on v2

--- a/solution.py
+++ b/solution.py
@@ -14,9 +14,9 @@
 
 
 def gather_rotate(
-    rows, cols, q, pheno, basis, kin, trait,
+    rows, cols, q, pheno, basis_in, kin_in, trait_in,
     gen_out, coeffs_out,
-    w_out, c_out, held, gen_sem, g, ph, acc, part_f, part, rparts, sb, rb, ob, crow, ct,
+    basis, kin, trait, w_out, c_out, held, gen_sem, g, ph, acc, part_f, part, rparts, sb, rb, ob, crow, ct,
     load_sem, send_sem, recv_sem, rs_send, rs_recv, a1_send, a1_recv, a2_send, a2_recv, ag_send, ag_recv,
 ):
     me_r, me_c = lax.axis_index("row"), lax.axis_index("col")
@@ -24,7 +24,7 @@
     z, y = me_c // 2, lax.rem(me_c, 2)
     other = me_c + 1 - 2 * y
     width, people = q.shape
-    piece = width // PIECES
+    piece = people // PIECES
     columns = pheno.shape[1]
     traits = basis.shape[0]
     sets = columns * cols // traits
@@ -34,6 +34,12 @@
     own_load.start()
     ph_load = pltpu.make_async_copy(pheno, ph, load_sem.at[1])
     ph_load.start()
+    small = [
+        pltpu.make_async_copy(a, b, load_sem.at[2 + i])
+        for i, (a, b) in enumerate(((basis_in, basis), (kin_in, kin), (trait_in, trait)))
+    ]
+    for copy in small:
+        copy.start()
 
     barrier = pltpu.get_barrier_semaphore()
     for d in range(1, cols):
@@ -44,7 +50,7 @@
 
     def hop(way, block, j):
         target = (jnp.minimum(me_c + 2, cols - 2 + y), jnp.maximum(me_c - 2, y), other)[way]
-        here = g.at[block, pl.ds(j * piece, piece)]
+        here = g.at[block, :, pl.ds(j * piece, piece)]
         return pltpu.make_async_remote_copy(
             src_ref=here, dst_ref=here,
             send_sem=send_sem.at[way, block, j], recv_sem=recv_sem.at[block, j],
@@ -71,37 +77,27 @@
         line_sends(me_c, j, lambda h: h.start())
         hop(2, me_c, j).start()
 
+    acc[...] = jnp.zeros_like(acc)
     ph_load.wait()
 
-    def project(pair):
-        acc[...] = jnp.zeros_like(acc)
-        step = 2048
-
-        def add(i, _):
-            at = pl.ds(pl.multiple_of(i * step, step), step)
-            lhs = jnp.concatenate([g[2 * pair, :, at], g[2 * pair + 1, :, at]], axis=0)
-            acc[...] += jnp.dot(lhs, ph[at, :], preferred_element_type=jnp.float32)
-            return 0
-
-        lax.fori_loop(0, people // step, add, 0)
-        part_f[...] = acc[...].T
-        for s in range(sets):
-            part[pair, s * t_here:(s + 1) * t_here, :] = part_f[pl.ds(s, t_here, stride=sets), :].astype(jnp.bfloat16)
-
+    def process(pair, j):
+        arrived(2 * pair + 1 - y, j)
+        lanes = pl.ds(pl.multiple_of(pair * LANES, LANES), LANES)
+        at = pl.ds(j * piece, piece)
+        lhs = jnp.concatenate([g[2 * pair, :, at], g[2 * pair + 1, :, at]], axis=0)
+        acc[pair] += jnp.dot(lhs, ph[at, :], preferred_element_type=jnp.float32)
+        w_out[at, lanes] = lhs.T
+
+    def by_set(s):
+        return part_f[pl.ds(s, t_here, stride=sets), :]
+
+    def finish_pair(pair):
         @pl.when(pair != me_r)
         def _():
+            part_f[...] = acc[pair].T
+            for s in range(sets):
+                part[pair, s * t_here:(s + 1) * t_here, :] = by_set(s).astype(jnp.bfloat16)
             reduce_copy(pair).start()
-
-    def lay(pair):
-        step = 512
-        lanes = pl.ds(pl.multiple_of(pair * LANES, LANES), LANES)
-
-        def turn(i, _):
-            at = pl.ds(pl.multiple_of(i * step, step), step)
-            w_out[at, lanes] = jnp.concatenate([g[2 * pair, :, at], g[2 * pair + 1, :, at]], axis=0).T
-            return 0
-
-        lax.fori_loop(0, people // step, turn, 0)
 
     def reduce_copy(pair):
         return pltpu.make_async_remote_copy(
@@ -110,22 +106,31 @@
             device_id=(pair, me_c), device_id_type=MESH,
         )
 
-    def wait_theirs(pair):
-        for j in range(PIECES):
-            arrived(2 * pair + 1 - y, j)
-
     def around(s, fn):
-        @pl.when(z - s >= 0)
-        def _():
-            fn(z - s)
-
-        @pl.when(z + s < lines)
-        def _():
-            fn(z + s)
-
-    def late_round(pair):
-        wait_theirs(pair)
-        project(pair)
+        if s == 0:
+            fn(z)
+            return
+
+        def side(i, _):
+            pair = z - s + 2 * s * i
+
+            @pl.when(jnp.logical_and(pair >= 0, pair < lines))
+            def _():
+                fn(pair)
+
+            return 0
+
+        lax.fori_loop(0, 2, side, 0)
+
+    order = [(0, j) for j in range(PIECES)] + [(1, j) for j in range(late)]
+    order += [(s, j) for s in range(2, lines) for j in range(PIECES)]
+    tail = [(1, j) for j in range(late, PIECES)]
+    done = 0
+
+    def handle(s, j):
+        around(s, lambda pair: process(pair, j))
+        if j == PIECES - 1:
+            around(s, finish_pair)
 
     for s in range(1, lines):
         for j in range(PIECES):
@@ -155,20 +160,20 @@
                 if not skip:
                     hop(2, b, j).start()
 
-        if s == 1:
-            wait_theirs(z)
-            project(z)
-            lay(z)
+            if (s, j) != (1, 0):
+                handle(*order[done])
+                done += 1
     for j in range(late, PIECES):
         line_sends(other, j, lambda h: h.start())
-    for s in range(2, lines - 1):
-        around(s, late_round)
-        around(s, lay)
-    for s in (lines - 1, 1):
-        around(s, late_round)
-    around(lines - 1, lay)
-
-    total = part[me_r].astype(jnp.float32)
+    rest = order[done:]
+    while rest or tail:
+        if rest and len(rest) > len(tail):
+            handle(*rest.pop(0))
+        else:
+            handle(*tail.pop(0))
+
+    part_f[...] = acc[me_r].T
+    total = jnp.concatenate([by_set(s) for s in range(sets)], axis=0)
     for d in range(1, rows):
         src = lax.rem(me_r + d, rows)
         pltpu.make_async_remote_copy(
@@ -201,7 +206,8 @@
     for p in col_peers:
         trade1(p, me_c).start()
     rb[me_c] = sb[me_c]
-    around(1, lay)
+    for copy in small:
+        copy.wait()
     product = kin[pl.ds(me_r, 1), :] * jnp.broadcast_to(trait[...], (LANES, traits)).T
     weight = product / (product + 1.0)
     for p in col_peers:
@@ -310,16 +316,19 @@
             jax.ShapeDtypeStruct((ind, columns), bf),
             jax.ShapeDtypeStruct((share, columns), f32),
         ),
-        in_specs=[hbm, hbm, vmem, vmem, vmem],
+        in_specs=[hbm] * 5,
         out_specs=(hbm, vmem),
         scratch_shapes=[
+            pltpu.VMEM((traits, traits), f32),
+            pltpu.VMEM((rows, share), f32),
+            pltpu.VMEM((1, traits), f32),
             pltpu.VMEM((ind, rows * share), bf),
             pltpu.VMEM((rows * share, columns), bf),
             pltpu.VMEM((ind, columns), bf),
             dma((16,)),
             pltpu.VMEM((cols, panel.shape[1], ind), bf),
             pltpu.VMEM((ind, columns), bf),
-            pltpu.VMEM((share, columns), f32),
+            pltpu.VMEM((cols // 2, share, columns), f32),
             pltpu.VMEM((columns, LANES), f32),
             pltpu.VMEM((rows, columns, LANES), bf),
             pltpu.VMEM((rows, columns, LANES), bf),
@@ -328,12 +337,12 @@
             pltpu.VMEM((cols, lot, LANES), bf),
             pltpu.VMEM((rows, cols, lot, LANES), bf),
             pltpu.VMEM((columns, LANES), f32),
-            dma((2,)), dma((3, cols, PIECES)), dma((cols, PIECES)),
+            dma((5,)), dma((3, cols, PIECES)), dma((cols, PIECES)),
             dma((rows,)), dma((rows,)), dma((cols,)), dma((cols,)), dma((cols,)), dma((cols,)),
             dma((rows,)), dma((rows,)),
         ],
         compiler_params=pltpu.CompilerParams(
-            collective_id=0, has_side_effects=True, vmem_limit_bytes=48 * 1024 * 1024
+            collective_id=0, has_side_effects=True, vmem_limit_bytes=56 * 1024 * 1024
         ),
     )(panel.T, pheno, trait_basis, kin_values.reshape(rows, share), trait_values[None, :])
     return coeffs, genetic

time: 119 us -> 118 us (level)
    unnamed x10 -> x2, local copies, waits for them, and re-layouts: 6.06 us -> 6.04 us
where the time goes in v3:
time: 118 us
  Pallas kernels  111 us (94%)
  local copies, waits for them, and re-layouts  6.04 us (5%)
    pallas_call x1, Pallas kernels, fused(): pl.pallas_call(functools.partial(gather_rotate, rows, cols), out_shape=(j...  111 us
    unnamed x2, local copies, waits for them, and re-layouts  6.04 us

profile of v3, /device:TPU:1, one launch (start us, length us, event | category | flops | bytes accessed | tf_op | source)
XLA Modules:
  0.0 118.1 jit_solution(9972045244094061172)
XLA Ops:
  0.6 111.4 %shard_map.68 = (bf16[8192,256]{1,0:T(8,128)(2,1)}, f32[128,256]{1,0:T(8,128)}) custom-call(bf16[64,8192]{1,0:T(8,128)(2,1)} %bitcast.3, bf16[8192,256]{1,0:T(8,128)(2,1)} %pheno.1, f32[128,128]{1,0:T(8,128)} %basis_in.1, f32[4,128]{1,0:T(4,128)} %bitcast.4, f32[1,128]{1,0:T(1,128)} %bitcast.5), custom_call_target="tpu_custom_call" | custom-call | tf_op jit(solution)/shard_map/pallas_call | solution.py:313
  112.1 1.6 %copy.9 = f32[128,256]{1,0:T(8,128)} copy(f32[128,256]{1,0:T(8,128)} %get-tuple-element.8) | data formatting | bytes 262144
  113.6 4.5 %copy.10 = bf16[8192,256]{1,0:T(8,128)(2,1)} copy(bf16[8192,256]{1,0:T(8,128)(2,1)} %get-tuple-element.9) | data formatting | bytes 8388608
